TPU v7x, 128 devices: a whole 4x4x4 slice. The times are simulated.
128 devices in a mesh: band: 8 (over x, core), grid: 16 (over z, y).
Axes of the slice: x: 4, y: 4, z: 4, core: 2. Of those that a mesh axis runs over, the one named last changes fastest.
Arguments:
- orbitals: bfloat16 [32768, 2048], P('grid', 'band'), may hold values from -6 to 6
- projectors: bfloat16 [128, 8, 128], replicated, may hold values from -0.5 to 0.5
- sphere_start: int32 [128], replicated, may hold values from 0 to 1920, as said below
- proj_count: int32 [128], replicated, may hold values from 1 to 8
- owner_slab: int32 [128], replicated, may hold values from 0 to 15, as said below
- correlation_coef: float32 [128, 8, 8], replicated, as said below
Outputs:
- rotated: bfloat16 [32768, 2048], P(('grid', 'band'))
Inputs may be any that keep to these rules, and one draw needn't show every extreme that they name: `sphere_start`: a multiple of 128. `owner_slab`: every slab owns exactly 8 atoms. `correlation_coef`: each atom's matrix is symmetric positive definite.
All inputs are finite; a program needn't handle non-finite values.
Results may differ from a plain program's by a relative error of at most 0.0049.
Values may be sent and summed in bfloat16 or wider, within the bound.
A program may use at most 128 MiB of HBM per device.

v0:
```python
import jax
import jax.numpy as jnp
from jax import lax
from jax.sharding import PartitionSpec as P

SPH = 128
NPMAX = 8
A_SLAB = 8


def inverse_factor(matrix):
    order = matrix.shape[0]
    if order <= 512 or order % 2 != 0:
        lower = jnp.linalg.cholesky(matrix)
        identity = jnp.eye(order, dtype=matrix.dtype)
        return lax.linalg.triangular_solve(lower, identity, left_side=True, lower=True)
    half = order // 2
    upper_inv = inverse_factor(matrix[:half, :half])
    below = jnp.dot(matrix[half:, :half], upper_inv.T, precision=lax.Precision.HIGHEST)
    schur = matrix[half:, half:] - jnp.dot(below, below.T, precision=lax.Precision.HIGHEST)
    lower_inv = inverse_factor(schur)
    corner = -jnp.dot(
        lower_inv,
        jnp.dot(below, upper_inv, precision=lax.Precision.HIGHEST),
        precision=lax.Precision.HIGHEST,
    )
    top = jnp.concatenate([upper_inv, jnp.zeros((half, order - half), matrix.dtype)], axis=1)
    bottom = jnp.concatenate([corner, lower_inv], axis=1)
    return jnp.concatenate([top, bottom], axis=0)


def slab_atoms(owner_slab, slab):
    atoms = owner_slab.shape[0]
    keyed = jnp.where(owner_slab == slab, 0, 1) * atoms + jnp.arange(atoms, dtype=jnp.int32)
    return jnp.argsort(keyed, stable=True)[:A_SLAB]


def atom_terms(source, weights, starts, counts, coefs, valid):

    def take_rows(offset):
        return lax.dynamic_slice_in_dim(source, offset, SPH, 0)

    sphere_rows = jax.vmap(take_rows)(starts)
    correlations = jnp.einsum(
        "aij,ajn->ain", weights, sphere_rows, preferred_element_type=jnp.float32
    )
    active = (jnp.arange(NPMAX)[None, :] < counts[:, None]) & valid[:, None]
    correlations = jnp.where(active[:, :, None], correlations, jnp.zeros_like(correlations))
    weighted = jnp.einsum("aij,ajn->ain", coefs, correlations, precision=lax.Precision.HIGHEST)
    return (correlations, weighted)


def shards(orbitals, projectors, sphere_start, proj_count, owner_slab, correlation_coef):
    band_index = lax.axis_index("band")
    slab = lax.axis_index("grid")
    nbands = lax.axis_size("band")
    total_rows = orbitals.shape[0] * lax.axis_size("grid")
    chosen = slab_atoms(owner_slab, slab)
    weights = projectors[chosen]
    counts = proj_count[chosen]
    coefs = correlation_coef[chosen]
    gathered = lax.all_gather(orbitals, "band", axis=1, tiled=True)
    width = orbitals.shape[1]
    width_all = gathered.shape[1]
    gram_panel = jnp.dot(orbitals.T, gathered, preferred_element_type=jnp.float32) * (
        1.0 / total_rows
    )
    valid = jnp.ones((A_SLAB,), dtype=bool)
    correlations, weighted = atom_terms(
        gathered, weights, sphere_start[chosen], counts, coefs, valid
    )
    panel_weighted = lax.dynamic_slice_in_dim(weighted, band_index * width, width, 2)
    paw = jnp.dot(
        panel_weighted.reshape(-1, width).T,
        correlations.reshape(-1, width_all),
        precision=lax.Precision.HIGHEST,
    )
    panel_total = lax.psum(gram_panel + paw, "grid")
    metric = lax.all_gather(panel_total, "band", axis=0, tiled=True)
    height = orbitals.shape[0] // nbands
    mine = lax.dynamic_slice_in_dim(gathered, band_index * height, height, 0)
    inverse = inverse_factor(metric).astype(jnp.bfloat16)
    return jnp.dot(mine, inverse.T, preferred_element_type=jnp.float32).astype(jnp.bfloat16)


def solution(mesh):
    in_specs = (P("grid", "band"), P(), P(), P(), P(), P())
    out_specs = P(("grid", "band"), None)
    return jax.shard_map(shards, mesh=mesh, in_specs=in_specs, out_specs=out_specs, check_vma=False)
```

profile of v0, /device:TPU:1, one launch (start us, length us, event | category | flops | bytes accessed | tf_op | source)
XLA Modules:
  0.0 1023.9 jit_solution(12298596556159580187)
XLA Ops:
  8.0 2.5 sort.17
  15.4 50.7 %all-gather.3.cloned.1.call-done = bf16[2048,2048]{1,0:T(8,128)(2,1)} async-done(((bf16[2048,256]{1,0:T(8,128)(2,1)}), bf16[2048,2048]{1,0:T(8,128)(2,1)}) %all-gather.3.cloned.1.call-update) | async-done | bytes 8388624 | tf_op jit(solution)/shard_map/all_gather | solution.py:62
  66.1 25.7 %while.9 = (s32[]{:T(128)}, bf16[2048,2048]{1,0:T(8,128)(2,1)}, s32[8,2]{0,1:T(2,128)S(1)}, bf16[8,128,2048]{2,1,0:T(8,128)(2,1)}, s32[]{:T(128)}) while((s32[]{:T(128)}, bf16[2048,2048]{1,0:T(8,128)(2,1)}, s32[8,2]{0,1:T(2,128)S(1)}, bf16[8,128,2048]{2,1,0:T(8,128)(2,1)}, s32[]{:T(128)}) %tuple.104), condition=%wide.while_cond.1, body=%wide.while_body.1.sunk | while | flops 2 | bytes 1049189 | solution.py:41
  66.7 2.6 bitcast_dynamic-update-slice_fusion.10
  69.8 2.6 bitcast_dynamic-update-slice_fusion.10
  73.1 2.6 bitcast_dynamic-update-slice_fusion.10
  76.3 2.6 bitcast_dynamic-update-slice_fusion.10
  79.5 2.6 bitcast_dynamic-update-slice_fusion.10
  82.7 2.6 bitcast_dynamic-update-slice_fusion.10
  85.9 2.6 bitcast_dynamic-update-slice_fusion.10
  89.1 2.6 bitcast_dynamic-update-slice_fusion.10
  91.7 2.9 convolution_select_fusion
  95.3 6.8 convolution_multiply_fusion
  102.0 3.2 fusion.12
  105.5 90.3 %all-reduce.7.cloned.1.call-done = f32[256,2048]{0,1:T(8,128)} async-done(((f32[256,2048]{0,1:T(8,128)}), f32[256,2048]{0,1:T(8,128)}) %all-reduce.7.cloned.1.call-update) | async-done | bytes 2097168 | tf_op jit(solution)/shard_map/psum | solution.py:78
  196.0 87.6 %all-gather.5.cloned.1.call-done = f32[2048,2048]{0,1:T(8,128)} async-done(((f32[256,2048]{0,1:T(8,128)}), f32[2048,2048]{0,1:T(8,128)}) %all-gather.5.cloned.1.call-update) | async-done | bytes 16777232 | tf_op jit(solution)/shard_map/all_gather | solution.py:79
  286.7 11.7 %cholesky.462 = f32[128,128]{1,0:T(8,128)S(1)} custom-call(f32[128,128]{1,0:T(8,128)S(1)} %cholesky.746), custom_call_target="Cholesky" | custom-call | tf_op jit(solution)/shard_map/jit(cholesky)/cholesky | solution.py:14
  298.6 9.8 custom-call.35
  309.1 11.7 %cholesky.481 = f32[128,128]{1,0:T(8,128)S(1)} custom-call(f32[128,128]{1,0:T(8,128)S(1)} %cholesky.750), custom_call_target="Cholesky" | custom-call | tf_op jit(solution)/shard_map/jit(cholesky)/cholesky | solution.py:14
  320.8 10.3 %custom-call.36 = f32[1,128,128]{1,2,0:T(8,128)S(1)} custom-call(f32[1,128,128]{2,1,0:T(8,128)S(1)} %get-tuple-element.131), custom_call_target="InvertDiagBlocksLowerTriangular" | custom-call | tf_op jit(solution)/shard_map/jit(cholesky)/cholesky | solution.py:14
  331.8 11.7 %cholesky.502 = f32[128,128]{1,0:T(8,128)S(1)} custom-call(f32[128,128]{1,0:T(8,128)S(1)} %cholesky.755), custom_call_target="Cholesky" | custom-call | tf_op jit(solution)/shard_map/jit(cholesky)/cholesky | solution.py:14
  343.5 9.8 custom-call.37
  353.9 11.7 %cholesky.519 = f32[128,128]{1,0:T(8,128)S(1)} custom-call(f32[128,128]{1,0:T(8,128)S(1)} %convolution_subtract_fusion.25), custom_call_target="Cholesky" | custom-call | tf_op jit(solution)/shard_map/jit(cholesky)/cholesky | solution.py:14
  370.5 7.6 while.10
  378.1 39.3 %custom-call.38 = f32[4,128,128]{1,2,0:T(8,128)S(1)} custom-call(f32[4,128,128]{2,1,0:T(8,128)S(1)} %get-tuple-element.43), custom_call_target="InvertDiagBlocksLowerTriangular" | custom-call | tf_op jit(solution)/shard_map/triangular_solve/custom-call.3 | solution.py:16
  421.7 4.7 fusion.19
  428.2 3.1 convolution_subtract_fusion.1
  435.1 12.1 %cholesky.534 = f32[128,128]{1,0:T(8,128)S(1)} custom-call(f32[128,128]{1,0:T(8,128)S(1)} %cholesky.759), custom_call_target="Cholesky" | custom-call | tf_op jit(solution)/shard_map/jit(cholesky)/cholesky | solution.py:14
  447.4 9.8 custom-call.39
  459.7 11.7 %cholesky.553 = f32[128,128]{1,0:T(8,128)S(1)} custom-call(f32[128,128]{1,0:T(8,128)S(1)} %cholesky.763), custom_call_target="Cholesky" | custom-call | tf_op jit(solution)/shard_map/jit(cholesky)/cholesky | solution.py:14
  471.5 9.8 custom-call.40
  482.8 11.9 %cholesky.574 = f32[128,128]{1,0:T(8,128)S(1)} custom-call(f32[128,128]{1,0:T(8,128)S(1)} %cholesky.768), custom_call_target="Cholesky" | custom-call | tf_op jit(solution)/shard_map/jit(cholesky)/cholesky | solution.py:14
  494.8 9.8 custom-call.41
  506.0 11.7 %cholesky.591 = f32[128,128]{1,0:T(8,128)S(1)} custom-call(f32[128,128]{1,0:T(8,128)S(1)} %convolution_subtract_fusion.24), custom_call_target="Cholesky" | custom-call | tf_op jit(solution)/shard_map/jit(cholesky)/cholesky | solution.py:14
  523.9 11.2 %while.11 = (s32[]{:T(128)}, f32[512,512]{1,0:T(8,128)}, s32[4,2]{0,1:T(2,128)S(1)}, f32[4,128,128]{2,1,0:T(8,128)S(1)}, s32[]{:T(128)}) while((s32[]{:T(128)}, f32[512,512]{1,0:T(8,128)}, s32[4,2]{0,1:T(2,128)S(1)}, f32[4,128,128]{2,1,0:T(8,128)S(1)}, s32[]{:T(128)}) %tuple.125), condition=%wide.while_cond.clone, body=%wide.while_body.clone.sunk | while | flops 2 | bytes 131189 | solution.py:16
  535.1 39.5 %custom-call.42 = f32[4,128,128]{1,2,0:T(8,128)S(1)} custom-call(f32[4,128,128]{2,1,0:T(8,128)S(1)} %get-tuple-element.44), custom_call_target="InvertDiagBlocksLowerTriangular" | custom-call | tf_op jit(solution)/shard_map/triangular_solve/custom-call.3 | solution.py:16
  583.3 7.0 fusion.173
  590.3 28.5 %fusion.9 = f32[1024,1024]{1,0:T(8,128)S(1)} fusion(f32[2048,2048]{0,1:T(8,128)} %all-gather.5.cloned.1.call-done, f32[512,512]{1,0:T(8,128)S(1)} %copy-done.5, f32[128,512]{1,0:T(8,128)S(1)} %fusion.125, f32[128,512]{1,0:T(8,128)S(1)} %fusion.126, f32[128,512]{1,0:T(8,128)S(1)} %fusion.128, f32[128,512]{1,0:T(8,128)S(1)} %fusion.81, ...), kind=kOutput, calls=%fused_computation.24 | convolution fusion | flops 12892241920 | bytes 11534336 | tf_op jit(solution)/shard_map/dot_general | solution.py:19
  618.8 18.2 %slice_subtract_fusion = f32[1024,1024]{0,1:T(8,128)} fusion(f32[2048,2048]{0,1:T(8,128)} %all-gather.5.cloned.1.call-done, f32[1024,1024]{1,0:T(8,128)S(1)} %fusion.9), kind=kOutput, calls=%fused_computation.26 | convolution fusion | flops 12885950464 | bytes 16777216 | tf_op jit(solution)/shard_map/dot_general | solution.py:20
  643.3 11.7 %cholesky.606 = f32[128,128]{1,0:T(8,128)S(1)} custom-call(f32[128,128]{1,0:T(8,128)S(1)} %cholesky.772), custom_call_target="Cholesky" | custom-call | tf_op jit(solution)/shard_map/jit(cholesky)/cholesky | solution.py:14
  655.2 9.8 custom-call.43
  667.5 11.7 %cholesky.625 = f32[128,128]{1,0:T(8,128)S(1)} custom-call(f32[128,128]{1,0:T(8,128)S(1)} %cholesky.776), custom_call_target="Cholesky" | custom-call | tf_op jit(solution)/shard_map/jit(cholesky)/cholesky | solution.py:14
  679.3 10.3 %custom-call.44 = f32[1,128,128]{1,2,0:T(8,128)S(1)} custom-call(f32[1,128,128]{2,1,0:T(8,128)S(1)} %get-tuple-element.111), custom_call_target="InvertDiagBlocksLowerTriangular" | custom-call | tf_op jit(solution)/shard_map/jit(cholesky)/cholesky | solution.py:14
  691.1 11.7 %cholesky.646 = f32[128,128]{1,0:T(8,128)S(1)} custom-call(f32[128,128]{1,0:T(8,128)S(1)} %cholesky.781), custom_call_target="Cholesky" | custom-call | tf_op jit(solution)/shard_map/jit(cholesky)/cholesky | solution.py:14
  702.9 9.8 custom-call.45
  714.1 11.7 %cholesky.663 = f32[128,128]{1,0:T(8,128)S(1)} custom-call(f32[128,128]{1,0:T(8,128)S(1)} %convolution_subtract_fusion.23), custom_call_target="Cholesky" | custom-call | tf_op jit(solution)/shard_map/jit(cholesky)/cholesky | solution.py:14
  732.4 11.7 %while.12 = (s32[]{:T(128)}, f32[512,512]{1,0:T(8,128)}, s32[4,2]{0,1:T(2,128)S(1)}, f32[4,128,128]{2,1,0:T(8,128)S(1)}, s32[]{:T(128)}) while((s32[]{:T(128)}, f32[512,512]{1,0:T(8,128)}, s32[4,2]{0,1:T(2,128)S(1)}, f32[4,128,128]{2,1,0:T(8,128)S(1)}, s32[]{:T(128)}) %tuple.126), condition=%wide.while_cond.clone.1, body=%wide.while_body.clone.1.sunk | while | flops 2 | bytes 131189 | solution.py:16
  744.1 39.3 %custom-call.46 = f32[4,128,128]{1,2,0:T(8,128)S(1)} custom-call(f32[4,128,128]{2,1,0:T(8,128)S(1)} %get-tuple-element.45), custom_call_target="InvertDiagBlocksLowerTriangular" | custom-call | tf_op jit(solution)/shard_map/triangular_solve/custom-call.3 | solution.py:16
  789.2 4.7 fusion.17
  794.0 3.3 convolution_subtract_fusion
  797.3 2.9 fusion.170
  801.2 17.2 %fusion.172 = f32[1024,1024]{1,0:T(8,128)} fusion(f32[1024,1024]{1,0:T(8,128)S(1)} %copy-done.17, f32[512,512]{1,0:T(8,128)S(1)} %copy-done.6, f32[128,512]{1,0:T(8,128)S(1)} %copy-done.12, f32[128,512]{1,0:T(8,128)S(1)} %fusion.126, f32[128,512]{1,0:T(8,128)S(1)} %fusion.128, f32[128,512]{1,0:T(8,128)S(1)} %fusion.81, f32[512,512]{1,0:T(8,128)S(1)} %copy-done.3), kind=kOutput, calls=%fused_computation.324 | convolution fusion | flops 12892241920 | bytes 11534336 | tf_op jit(solution)/shard_map/dot_general | solution.py:24
  822.1 11.7 %cholesky.678 = f32[128,128]{1,0:T(8,128)S(1)} custom-call(f32[128,128]{1,0:T(8,128)S(1)} %cholesky.785), custom_call_target="Cholesky" | custom-call | tf_op jit(solution)/shard_map/jit(cholesky)/cholesky | solution.py:14
  834.0 9.8 custom-call.47
  846.4 11.7 %cholesky.697 = f32[128,128]{1,0:T(8,128)S(1)} custom-call(f32[128,128]{1,0:T(8,128)S(1)} %cholesky.789), custom_call_target="Cholesky" | custom-call | tf_op jit(solution)/shard_map/jit(cholesky)/cholesky | solution.py:14
  858.1 10.0 custom-call.48
  869.6 11.7 %cholesky.718 = f32[128,128]{1,0:T(8,128)S(1)} custom-call(f32[128,128]{1,0:T(8,128)S(1)} %cholesky.794), custom_call_target="Cholesky" | custom-call | tf_op jit(solution)/shard_map/jit(cholesky)/cholesky | solution.py:14
  881.4 9.8 custom-call.49
  892.6 11.7 %cholesky.735 = f32[128,128]{1,0:T(8,128)S(1)} custom-call(f32[128,128]{1,0:T(8,128)S(1)} %convolution_subtract_fusion.22), custom_call_target="Cholesky" | custom-call | tf_op jit(solution)/shard_map/jit(cholesky)/cholesky | solution.py:14
  911.2 12.0 %while.13 = (s32[]{:T(128)}, f32[512,512]{1,0:T(8,128)}, s32[4,2]{0,1:T(2,128)S(1)}, f32[4,128,128]{2,1,0:T(8,128)S(1)}, s32[]{:T(128)}) while((s32[]{:T(128)}, f32[512,512]{1,0:T(8,128)}, s32[4,2]{0,1:T(2,128)S(1)}, f32[4,128,128]{2,1,0:T(8,128)S(1)}, s32[]{:T(128)}) %tuple.127), condition=%wide.while_cond.clone.2, body=%wide.while_body.clone.2.sunk | while | flops 2 | bytes 131189 | solution.py:16
  923.2 39.3 %custom-call.50 = f32[4,128,128]{1,2,0:T(8,128)S(1)} custom-call(f32[4,128,128]{2,1,0:T(8,128)S(1)} %get-tuple-element.46), custom_call_target="InvertDiagBlocksLowerTriangular" | custom-call | tf_op jit(solution)/shard_map/triangular_solve/custom-call.3 | solution.py:16
  970.3 6.0 fusion.16
  976.3 13.6 %negate_convert_fusion = bf16[1024,1024]{1,0:T(8,128)(2,1)S(1)} fusion(f32[1024,1024]{1,0:T(8,128)S(1)} %copy-done.18, f32[512,512]{1,0:T(8,128)S(1)} %copy-done.7, f32[128,512]{1,0:T(8,128)S(1)} %fusion.113, f32[128,512]{1,0:T(8,128)S(1)} %fusion.114, f32[128,512]{1,0:T(8,128)S(1)} %fusion.116, f32[128,512]{1,0:T(8,128)S(1)} %fusion.77, ...), kind=kOutput, calls=%fused_computation.30 | convolution fusion | flops 12894339072 | bytes 9437184 | tf_op jit(solution)/shard_map/dot_general | solution.py:22
  990.0 26.9 %fusion.13 = bf16[256,2048]{1,0:T(8,128)(2,1)} fusion(bf16[1024,1024]{1,0:T(8,128)(2,1)S(1)} %copy-done.13, bf16[1024,1024]{1,0:T(8,128)(2,1)S(1)} %fusion.16, bf16[1024,1024]{1,0:T(8,128)(2,1)S(1)} %negate_convert_fusion, bf16[2048,2048]{1,0:T(8,128)(2,1)} %get-tuple-element.377, s32[]{:T(128)S(6)} %select_n.31), kind=kOutput, calls=%fused_computation.34 | convolution fusion | flops 2181562368 | bytes 8388612 | tf_op jit(solution)/shard_map/dot_general | solution.py:83
  (247 shorter events, 133.2 us)
Async XLA Ops:
  6.5 4.0 copy-start
  6.5 59.5 %all-gather.3.cloned.1.call-start = ((), (), s32[]{:S(2)}) async-start(), calls=%async_computation | async-start | bytes 9437184 | tf_op jit(solution)/shard_map/all_gather | solution.py:62
  7.3 188.6 %all-reduce.7.cloned.1.call-start = ((), (), s32[]{:S(2)}) async-start(), calls=%async_computation.1 | async-start | bytes 4194304 | tf_op jit(solution)/shard_map/psum | solution.py:78
  91.7 3.5 copy-start.14
  105.3 178.4 %all-gather.5.cloned.1.call-start = ((), (), s32[]{:S(2)}) async-start(), calls=%async_computation.2 | async-start | bytes 18874368 | tf_op jit(solution)/shard_map/all_gather | solution.py:79
  434.1 1.0 copy-start.8
  574.7 3.5 copy-start.15
  575.1 8.2 copy-start.5
  581.4 8.8 copy-start.11
  583.3 35.5 %copy-start.2 = (f32[512,512]{1,0:T(8,128)}, f32[512,512]{1,0:T(8,128)S(1)}, u32[]{:S(2)}) copy-start(f32[512,512]{1,0:T(8,128)S(1)} %convolution_negate_fusion.1) | copy-start | bytes 3145732
  618.8 18.2 %copy-start.16 = (f32[1024,1024]{1,0:T(8,128)}, f32[1024,1024]{1,0:T(8,128)S(1)}, u32[]{:S(2)}) copy-start(f32[1024,1024]{1,0:T(8,128)S(1)} %fusion.9) | copy-start | bytes 12582916
  642.3 1.0 copy-start.10
  793.9 7.3 copy-start.3
  794.0 7.3 copy-start.6
  794.0 7.2 copy-start.12
  794.0 7.2 copy-start.17
  821.1 1.0 copy-start.9
  909.8 58.6 %copy-start.4 = (f32[512,512]{1,0:T(8,128)S(1)}, f32[512,512]{1,0:T(8,128)}, u32[]{:S(2)}) copy-start(f32[512,512]{1,0:T(8,128)} %fusion.170) | copy-start | bytes 3145732
  962.9 7.4 copy-start.7
  968.5 7.9 copy-start.18
  976.3 13.7 %copy-start.13 = (bf16[1024,1024]{1,0:T(8,128)(2,1)S(1)}, bf16[1024,1024]{1,0:T(8,128)(2,1)}, u32[]{:S(2)}) copy-start(bf16[1024,1024]{1,0:T(8,128)(2,1)} %fusion.173) | copy-start | bytes 6291460
  990.0 26.9 %copy-start.1 = (bf16[128,8,128]{2,1,0:T(8,128)(2,1)S(1)}, bf16[128,8,128]{2,1,0:T(8,128)(2,1)}, u32[]{:S(2)}) copy-start(bf16[128,8,128]{2,1,0:T(8,128)(2,1)} %param.10) | copy-start | bytes 786436
Sparse Core Ops, SparseCore 0:
  9.0 57.0 all-gather.2
  105.4 90.4 all-reduce.6
  197.6 86.0 all-gather.4
where the time goes:
time: 1030 us; the launch traced here: 1020 us
  other arithmetic  503 us (49%)
  waiting for transfers between devices  229 us (22%)
  matrix products  182 us (18%)
  local copies, waits for them, and re-layouts  84.3 us (8%)
  between operations  25.2 us (2%)
    another operation x59, other arithmetic, inverse_factor(): lower = jnp.linalg.cholesky(matrix)  317 us
    another operation x11, other arithmetic, inverse_factor(): lax.linalg.triangular_solve(lower, identity, left_side=True, lower=True)  163 us
    psum x1, waiting for transfers between devices, shards(): panel_total = lax.psum(gram_panel + paw, 'grid')  90.3 us
    all_gather x1, waiting for transfers between devices, shards(): metric = lax.all_gather(panel_total, 'band', axis=0, tiled=True)  87.6 us
    all_gather x1, waiting for transfers between devices, shards(): gathered = lax.all_gather(orbitals, 'band', axis=1, tiled=True)  50.7 us
    another operation x53, local copies, waits for them, and re-layouts, inverse_factor(): lax.linalg.triangular_solve(lower, identity, left_side=True, lower=True)  42.3 us
    dot_general x3, matrix products, inverse_factor(): jnp.dot(matrix[half:, :half], upper_inv.T, precision=lax.Precision.HIGHEST)  38 us
    dot_general x1, matrix products, shards(): jnp.dot(mine, inverse.T, preferred_element_type=jnp.float32)  26.9 us
  transfers between devices with their start and end apart: 3, of which 3 were waited for; matrix products, arithmetic and copies ran while one was open for 1% of the time, Pallas kernels for 0%

commit v1 on v0

--- a/solution.py
+++ b/solution.py
@@ -6,6 +6,19 @@
 SPH = 128
 NPMAX = 8
 A_SLAB = 8
+
+
+def run_lines(frame):
+    current_value = jnp.concatenate(
+        lax.all_to_all(
+            jnp.stack(lax.axis_size("band") * [frame]),
+            axis_name="band",
+            split_axis=0,
+            concat_axis=0,
+        ),
+        axis=0,
+    )
+    return current_value
 
 
 def inverse_factor(matrix):
@@ -76,7 +89,7 @@
         precision=lax.Precision.HIGHEST,
     )
     panel_total = lax.psum(gram_panel + paw, "grid")
-    metric = lax.all_gather(panel_total, "band", axis=0, tiled=True)
+    metric = run_lines(panel_total)
     height = orbitals.shape[0] // nbands
     mine = lax.dynamic_slice_in_dim(gathered, band_index * height, height, 0)
     inverse = inverse_factor(metric).astype(jnp.bfloat16)

time: 1030 us -> 1150 us (1.12)
  waiting for transfers between devices: 229 us -> 325 us
  local copies, waits for them, and re-layouts: 84.3 us -> 107 us
    all_to_all x0 -> x1, waiting for transfers between devices: none -> 184 us  [run_lines(): lax.all_to_all(jnp.stack(lax.axis_size('band') * [frame]), axis_name='ban...]
    all_gather x1 -> x0, waiting for transfers between devices: 87.6 us -> none  [shards(): metric = lax.all_gather(panel_total, 'band', axis=0, tiled=True)]
where the time goes in v1:
time: 1150 us; the launch traced here: 1140 us
  other arithmetic  503 us (44%)
  waiting for transfers between devices  325 us (28%)
  matrix products  173 us (15%)
  local copies, waits for them, and re-layouts  107 us (9%)
  between operations  25.6 us (2%)
    another operation x59, other arithmetic, inverse_factor(): lower = jnp.linalg.cholesky(matrix)  317 us
    all_to_all x1, waiting for transfers between devices, run_lines(): lax.all_to_all(jnp.stack(lax.axis_size('band') * [frame]), axis_name='ban...  184 us
    another operation x11, other arithmetic, inverse_factor(): lax.linalg.triangular_solve(lower, identity, left_side=True, lower=True)  163 us
    psum x1, waiting for transfers between devices, shards(): panel_total = lax.psum(gram_panel + paw, 'grid')  90.6 us
    all_gather x1, waiting for transfers between devices, shards(): gathered = lax.all_gather(orbitals, 'band', axis=1, tiled=True)  50.7 us
    another operation x53, local copies, waits for them, and re-layouts, inverse_factor(): lax.linalg.triangular_solve(lower, identity, left_side=True, lower=True)  43.5 us
    dot_general x3, matrix products, inverse_factor(): jnp.dot(matrix[half:, :half], upper_inv.T, precision=lax.Precision.HIGHEST)  36.9 us
    dot_general x1, matrix products, shards(): jnp.dot(mine, inverse.T, preferred_element_type=jnp.float32)  26.8 us
  transfers between devices with their start and end apart: 3, of which 3 were waited for; matrix products, arithmetic and copies ran while one was open for 1% of the time, Pallas kernels for 0%

profile of v1, /device:TPU:1, one launch (start us, length us, event | category | flops | bytes accessed | tf_op | source)
XLA Modules:
  0.0 1141.9 jit_solution(14004281755383319010)
XLA Ops:
  15.4 50.7 %all-gather.2.cloned.1.call-done = bf16[2048,2048]{1,0:T(8,128)(2,1)} async-done(((bf16[2048,256]{1,0:T(8,128)(2,1)}), bf16[2048,2048]{1,0:T(8,128)(2,1)}) %all-gather.2.cloned.1.call-update) | async-done | bytes 8388624 | tf_op jit(solution)/shard_map/all_gather | solution.py:75
  66.1 25.9 %while.9 = (s32[]{:T(128)}, bf16[2048,2048]{1,0:T(8,128)(2,1)}, s32[8,2]{0,1:T(2,128)S(1)}, bf16[8,128,2048]{2,1,0:T(8,128)(2,1)}, s32[]{:T(128)}) while((s32[]{:T(128)}, bf16[2048,2048]{1,0:T(8,128)(2,1)}, s32[8,2]{0,1:T(2,128)S(1)}, bf16[8,128,2048]{2,1,0:T(8,128)(2,1)}, s32[]{:T(128)}) %tuple.104), condition=%wide.while_cond.1, body=%wide.while_body.1.sunk | while | flops 2 | bytes 1049689 | solution.py:54
  66.6 2.6 bitcast_dynamic-update-slice_fusion.10
  69.9 2.6 bitcast_dynamic-update-slice_fusion.10
  73.1 2.7 bitcast_dynamic-update-slice_fusion.10
  76.3 2.7 bitcast_dynamic-update-slice_fusion.10
  79.6 2.6 bitcast_dynamic-update-slice_fusion.10
  82.8 2.7 bitcast_dynamic-update-slice_fusion.10
  89.3 2.7 bitcast_dynamic-update-slice_fusion.10
  91.9 3.0 convolution_select_fusion
  97.4 3.6 fusion.12
  101.0 90.6 %all-reduce.7.cloned.1.call-done = f32[256,2048]{1,0:T(8,128)} async-done(((f32[256,2048]{1,0:T(8,128)}), f32[256,2048]{1,0:T(8,128)}) %all-reduce.7.cloned.1.call-update) | async-done | bytes 2097168 | tf_op jit(solution)/shard_map/psum | solution.py:91
  193.5 7.2 stack.2
  200.7 7.7 all-to-all-start
  208.5 183.5 %all-to-all-done = f32[8,256,2048]{1,2,0:T(8,128)} async-done(((f32[8,256,2048]{1,2,0:T(8,128)}), f32[8,256,2048]{1,2,0:T(8,128)}, u32[]{:S(2)}, u32[]{:S(2)}) %all-to-all-start) | async-done | bytes 16777248 | tf_op jit(solution)/shard_map/all_to_all | solution.py:13
  392.0 7.3 copy.47
  399.4 5.7 copy-done.3
  407.0 11.7 %cholesky.462 = f32[128,128]{1,0:T(8,128)S(1)} custom-call(f32[128,128]{1,0:T(8,128)S(1)} %cholesky.746), custom_call_target="Cholesky" | custom-call | tf_op jit(solution)/shard_map/jit(cholesky)/cholesky | solution.py:27
  418.7 9.8 custom-call.35
  429.3 11.7 %cholesky.481 = f32[128,128]{1,0:T(8,128)S(1)} custom-call(f32[128,128]{1,0:T(8,128)S(1)} %cholesky.750), custom_call_target="Cholesky" | custom-call | tf_op jit(solution)/shard_map/jit(cholesky)/cholesky | solution.py:27
  441.1 10.2 custom-call.36
  451.9 11.7 %cholesky.502 = f32[128,128]{1,0:T(8,128)S(1)} custom-call(f32[128,128]{1,0:T(8,128)S(1)} %cholesky.755), custom_call_target="Cholesky" | custom-call | tf_op jit(solution)/shard_map/jit(cholesky)/cholesky | solution.py:27
  464.3 9.8 custom-call.37
  474.7 11.7 %cholesky.519 = f32[128,128]{1,0:T(8,128)S(1)} custom-call(f32[128,128]{1,0:T(8,128)S(1)} %convolution_subtract_fusion.25), custom_call_target="Cholesky" | custom-call | tf_op jit(solution)/shard_map/jit(cholesky)/cholesky | solution.py:27
  490.7 8.1 while.10
  498.8 39.3 %custom-call.38 = f32[4,128,128]{1,2,0:T(8,128)S(1)} custom-call(f32[4,128,128]{2,1,0:T(8,128)S(1)} %get-tuple-element.43), custom_call_target="InvertDiagBlocksLowerTriangular" | custom-call | tf_op jit(solution)/shard_map/triangular_solve/custom-call.3 | solution.py:29
  542.5 4.7 fusion.19
  549.0 3.1 convolution_subtract_fusion.1
  555.9 12.1 %cholesky.534 = f32[128,128]{1,0:T(8,128)S(1)} custom-call(f32[128,128]{1,0:T(8,128)S(1)} %cholesky.759), custom_call_target="Cholesky" | custom-call | tf_op jit(solution)/shard_map/jit(cholesky)/cholesky | solution.py:27
  568.2 9.8 custom-call.39
  580.5 11.7 %cholesky.553 = f32[128,128]{1,0:T(8,128)S(1)} custom-call(f32[128,128]{1,0:T(8,128)S(1)} %cholesky.763), custom_call_target="Cholesky" | custom-call | tf_op jit(solution)/shard_map/jit(cholesky)/cholesky | solution.py:27
  593.7 9.8 custom-call.40
  605.1 11.9 %cholesky.574 = f32[128,128]{1,0:T(8,128)S(1)} custom-call(f32[128,128]{1,0:T(8,128)S(1)} %cholesky.768), custom_call_target="Cholesky" | custom-call | tf_op jit(solution)/shard_map/jit(cholesky)/cholesky | solution.py:27
  617.7 9.8 custom-call.41
  628.9 11.7 %cholesky.591 = f32[128,128]{1,0:T(8,128)S(1)} custom-call(f32[128,128]{1,0:T(8,128)S(1)} %convolution_subtract_fusion.24), custom_call_target="Cholesky" | custom-call | tf_op jit(solution)/shard_map/jit(cholesky)/cholesky | solution.py:27
  645.1 12.0 %while.11 = (s32[]{:T(128)}, f32[512,512]{1,0:T(8,128)}, s32[4,2]{0,1:T(2,128)S(1)}, f32[4,128,128]{2,1,0:T(8,128)S(1)}, s32[]{:T(128)}) while((s32[]{:T(128)}, f32[512,512]{1,0:T(8,128)}, s32[4,2]{0,1:T(2,128)S(1)}, f32[4,128,128]{2,1,0:T(8,128)S(1)}, s32[]{:T(128)}) %tuple.123), condition=%wide.while_cond.clone, body=%wide.while_body.clone.sunk | while | flops 2 | bytes 131181 | solution.py:29
  657.1 39.3 %custom-call.42 = f32[4,128,128]{1,2,0:T(8,128)S(1)} custom-call(f32[4,128,128]{2,1,0:T(8,128)S(1)} %get-tuple-element.44), custom_call_target="InvertDiagBlocksLowerTriangular" | custom-call | tf_op jit(solution)/shard_map/triangular_solve/custom-call.3 | solution.py:29
  705.1 28.6 %fusion.9 = f32[1024,1024]{1,0:T(8,128)S(1)} fusion(f32[2048,2048]{0,1:T(8,128)} %bitcast.228, f32[512,512]{1,0:T(8,128)S(1)} %copy-done.8, f32[128,512]{1,0:T(8,128)S(1)} %fusion.125, f32[128,512]{1,0:T(8,128)S(1)} %fusion.126, f32[128,512]{1,0:T(8,128)S(1)} %fusion.128, f32[128,512]{1,0:T(8,128)S(1)} %fusion.81, f32[512,512]{1,0:T(8,128)S(1)} %convolution_negate_fusion.1), kind=kOutput, calls=%fused_computation.24 | convolution fusion | flops 12892241920 | bytes 11534336 | tf_op jit(solution)/shard_map/dot_general | solution.py:32
  733.8 16.8 %fusion.172 = f32[1024,1024]{1,0:T(8,128)} fusion(f32[1024,1024]{1,0:T(8,128)S(1)} %fusion.9, f32[512,512]{1,0:T(8,128)S(1)} %copy-done.8, f32[128,512]{1,0:T(8,128)S(1)} %fusion.125, f32[128,512]{1,0:T(8,128)S(1)} %fusion.126, f32[128,512]{1,0:T(8,128)S(1)} %fusion.128, f32[128,512]{1,0:T(8,128)S(1)} %fusion.81, f32[512,512]{1,0:T(8,128)S(1)} %convolution_negate_fusion.1), kind=kOutput, calls=%fused_computation.324 | convolution fusion | flops 12892241920 | bytes 11534336 | tf_op jit(solution)/shard_map/dot_general | solution.py:37
  750.5 16.0 %slice_subtract_fusion = f32[1024,1024]{0,1:T(8,128)S(1)} fusion(f32[2048,2048]{0,1:T(8,128)} %bitcast.229, f32[1024,1024]{1,0:T(8,128)S(1)} %fusion.9), kind=kOutput, calls=%fused_computation.26 | convolution fusion | flops 12885950464 | bytes 16777216 | tf_op jit(solution)/shard_map/dot_general | solution.py:33
  773.6 11.7 %cholesky.606 = f32[128,128]{1,0:T(8,128)S(1)} custom-call(f32[128,128]{1,0:T(8,128)S(1)} %cholesky.772), custom_call_target="Cholesky" | custom-call | tf_op jit(solution)/shard_map/jit(cholesky)/cholesky | solution.py:27
  785.5 9.8 custom-call.43
  797.8 11.7 %cholesky.625 = f32[128,128]{1,0:T(8,128)S(1)} custom-call(f32[128,128]{1,0:T(8,128)S(1)} %cholesky.776), custom_call_target="Cholesky" | custom-call | tf_op jit(solution)/shard_map/jit(cholesky)/cholesky | solution.py:27
  810.9 10.0 custom-call.44
  822.5 11.7 %cholesky.646 = f32[128,128]{1,0:T(8,128)S(1)} custom-call(f32[128,128]{1,0:T(8,128)S(1)} %cholesky.781), custom_call_target="Cholesky" | custom-call | tf_op jit(solution)/shard_map/jit(cholesky)/cholesky | solution.py:27
  834.9 9.8 custom-call.45
  846.2 11.7 %cholesky.663 = f32[128,128]{1,0:T(8,128)S(1)} custom-call(f32[128,128]{1,0:T(8,128)S(1)} %convolution_subtract_fusion.23), custom_call_target="Cholesky" | custom-call | tf_op jit(solution)/shard_map/jit(cholesky)/cholesky | solution.py:27
  862.8 11.8 %while.12 = (s32[]{:T(128)}, f32[512,512]{1,0:T(8,128)}, s32[4,2]{0,1:T(2,128)S(1)}, f32[4,128,128]{2,1,0:T(8,128)S(1)}, s32[]{:T(128)}) while((s32[]{:T(128)}, f32[512,512]{1,0:T(8,128)}, s32[4,2]{0,1:T(2,128)S(1)}, f32[4,128,128]{2,1,0:T(8,128)S(1)}, s32[]{:T(128)}) %tuple.124), condition=%wide.while_cond.clone.1, body=%wide.while_body.clone.1.sunk | while | flops 2 | bytes 131181 | solution.py:29
  874.7 39.3 %custom-call.46 = f32[4,128,128]{1,2,0:T(8,128)S(1)} custom-call(f32[4,128,128]{2,1,0:T(8,128)S(1)} %get-tuple-element.45), custom_call_target="InvertDiagBlocksLowerTriangular" | custom-call | tf_op jit(solution)/shard_map/triangular_solve/custom-call.3 | solution.py:29
  921.1 3.6 fusion.17
  924.7 2.9 fusion.170
  929.5 7.1 fusion.173
  940.3 11.7 %cholesky.678 = f32[128,128]{1,0:T(8,128)S(1)} custom-call(f32[128,128]{1,0:T(8,128)S(1)} %cholesky.785), custom_call_target="Cholesky" | custom-call | tf_op jit(solution)/shard_map/jit(cholesky)/cholesky | solution.py:27
  952.2 9.8 custom-call.47
  964.6 11.7 %cholesky.697 = f32[128,128]{1,0:T(8,128)S(1)} custom-call(f32[128,128]{1,0:T(8,128)S(1)} %cholesky.789), custom_call_target="Cholesky" | custom-call | tf_op jit(solution)/shard_map/jit(cholesky)/cholesky | solution.py:27
  977.7 10.2 custom-call.48
  989.4 11.7 %cholesky.718 = f32[128,128]{1,0:T(8,128)S(1)} custom-call(f32[128,128]{1,0:T(8,128)S(1)} %cholesky.794), custom_call_target="Cholesky" | custom-call | tf_op jit(solution)/shard_map/jit(cholesky)/cholesky | solution.py:27
  1001.9 9.8 custom-call.49
  1013.1 11.7 %cholesky.735 = f32[128,128]{1,0:T(8,128)S(1)} custom-call(f32[128,128]{1,0:T(8,128)S(1)} %convolution_subtract_fusion.22), custom_call_target="Cholesky" | custom-call | tf_op jit(solution)/shard_map/jit(cholesky)/cholesky | solution.py:27
  1029.4 11.8 %while.13 = (s32[]{:T(128)}, f32[512,512]{1,0:T(8,128)}, s32[4,2]{0,1:T(2,128)S(1)}, f32[4,128,128]{2,1,0:T(8,128)S(1)}, s32[]{:T(128)}) while((s32[]{:T(128)}, f32[512,512]{1,0:T(8,128)}, s32[4,2]{0,1:T(2,128)S(1)}, f32[4,128,128]{2,1,0:T(8,128)S(1)}, s32[]{:T(128)}) %tuple.125), condition=%wide.while_cond.clone.2, body=%wide.while_body.clone.2.sunk | while | flops 2 | bytes 131181 | solution.py:29
  1041.2 39.3 %custom-call.50 = f32[4,128,128]{1,2,0:T(8,128)S(1)} custom-call(f32[4,128,128]{2,1,0:T(8,128)S(1)} %get-tuple-element.46), custom_call_target="InvertDiagBlocksLowerTriangular" | custom-call | tf_op jit(solution)/shard_map/triangular_solve/custom-call.3 | solution.py:29
  1088.3 6.0 fusion.16
  1094.3 13.6 %negate_convert_fusion = bf16[1024,1024]{1,0:T(8,128)(2,1)S(1)} fusion(f32[1024,1024]{1,0:T(8,128)S(1)} %copy-done.20, f32[512,512]{1,0:T(8,128)S(1)} %copy-done.10, f32[128,512]{1,0:T(8,128)S(1)} %fusion.113, f32[128,512]{1,0:T(8,128)S(1)} %fusion.114, f32[128,512]{1,0:T(8,128)S(1)} %fusion.116, f32[128,512]{1,0:T(8,128)S(1)} %fusion.77, ...), kind=kOutput, calls=%fused_computation.30 | convolution fusion | flops 12894339072 | bytes 9437184 | tf_op jit(solution)/shard_map/dot_general | solution.py:35
  1107.9 26.8 %fusion.13 = bf16[256,2048]{1,0:T(8,128)(2,1)} fusion(bf16[1024,1024]{1,0:T(8,128)(2,1)S(1)} %copy-done.18, bf16[1024,1024]{1,0:T(8,128)(2,1)S(1)} %fusion.16, bf16[1024,1024]{1,0:T(8,128)(2,1)S(1)} %negate_convert_fusion, bf16[2048,2048]{1,0:T(8,128)(2,1)} %get-tuple-element.366, s32[]{:T(128)S(6)} %select_n.31), kind=kOutput, calls=%fused_computation.34 | convolution fusion | flops 2181562368 | bytes 8388612 | tf_op jit(solution)/shard_map/dot_general | solution.py:96
  (253 shorter events, 145.1 us)
Async XLA Ops:
  6.5 5.3 copy-start
  6.5 59.5 %all-gather.2.cloned.1.call-start = ((), (), s32[]{:S(2)}) async-start(), calls=%async_computation.1 | async-start | bytes 9437184 | tf_op jit(solution)/shard_map/all_gather | solution.py:75
  7.3 184.4 %all-reduce.7.cloned.1.call-start = ((), (), s32[]{:S(2)}) async-start(), calls=%async_computation.2 | async-start | bytes 4194304 | tf_op jit(solution)/shard_map/psum | solution.py:91
  91.9 5.4 copy-start.2
  94.9 2.5 copy-start.4
  200.7 191.3 %all-to-all-start = ((f32[8,256,2048]{1,2,0:T(8,128)}), f32[8,256,2048]{1,2,0:T(8,128)}, u32[]{:S(2)}, u32[]{:S(2)}) async-start(f32[8,256,2048]{1,2,0:T(8,128)} %stack.2), calls=%async_computation | async-start | bytes 33554432 | tf_op jit(solution)/shard_map/all_to_all | solution.py:13
  399.4 5.7 copy-start.3
  554.9 1.0 copy-start.13
  696.4 3.5 copy-start.19
  696.9 8.2 copy-start.8
  703.2 30.5 %copy-start.16 = (f32[128,512]{1,0:T(8,128)}, f32[128,512]{1,0:T(8,128)S(1)}, u32[]{:S(2)}) copy-start(f32[128,512]{1,0:T(8,128)S(1)} %fusion.125) | copy-start | bytes 786436
  705.1 28.7 %copy-start.5 = (f32[512,512]{1,0:T(8,128)}, f32[512,512]{1,0:T(8,128)S(1)}, u32[]{:S(2)}) copy-start(f32[512,512]{1,0:T(8,128)S(1)} %convolution_negate_fusion.1) | copy-start | bytes 3145732
  766.6 2.0 copy-start.11
  772.6 1.0 copy-start.15
  914.0 7.1 copy-start.12
  924.6 4.8 copy-start.6
  924.6 4.8 copy-start.9
  924.7 4.8 copy-start.17
  939.4 1.0 copy-start.14
  1028.1 58.3 %copy-start.7 = (f32[512,512]{1,0:T(8,128)S(1)}, f32[512,512]{1,0:T(8,128)}, u32[]{:S(2)}) copy-start(f32[512,512]{1,0:T(8,128)} %fusion.170) | copy-start | bytes 3145732
  1080.9 7.4 copy-start.10
  1086.4 7.9 copy-start.20
  1094.3 13.6 %copy-start.18 = (bf16[1024,1024]{1,0:T(8,128)(2,1)S(1)}, bf16[1024,1024]{1,0:T(8,128)(2,1)}, u32[]{:S(2)}) copy-start(bf16[1024,1024]{1,0:T(8,128)(2,1)} %fusion.173) | copy-start | bytes 6291460
  1107.9 26.8 %copy-start.1 = (bf16[128,8,128]{2,1,0:T(8,128)(2,1)S(1)}, bf16[128,8,128]{2,1,0:T(8,128)(2,1)}, u32[]{:S(2)}) copy-start(bf16[128,8,128]{2,1,0:T(8,128)(2,1)} %param.10) | copy-start | bytes 786436
Sparse Core Ops, SparseCore 0:
  9.0 57.0 all-gather.1
  101.2 90.4 all-reduce.6
